TPU v7x, 32 devices: a whole 2x2x4 slice. The times are simulated.
32 devices in a mesh: edp: 2 (over y), ep: 16 (over z, x, core).
Axes of the slice: x: 2, y: 2, z: 4, core: 2. Of those that a mesh axis runs over, the one named last changes fastest.
Arguments:
- tokens: bfloat16 [4096, 2048], P(('edp', 'ep')), may hold values from -6 to 6
- routes: int32 [4096, 8], P(('edp', 'ep')), may hold values from 0 to 15, all different within a row; in each aligned block of 128 rows (0 to 127, 128 to 255, ...) at most 96 rows name the same one
- gate_weights: float32 [4096, 8], P(('edp', 'ep')), may hold values from 0.05 to 0.5
- w_gate: bfloat16 [16, 2048, 768], P('ep'), may hold values from -0.125 to 0.125
- w_up: bfloat16 [16, 2048, 768], P('ep'), may hold values from -0.125 to 0.125
- w_down: bfloat16 [16, 768, 2048], P('ep'), may hold values from -0.21875 to 0.21875
- saved_inputs: bfloat16 [16, 512, 2048], P('ep', 'edp'), may hold values from -6 to 6
- saved_cotangent: bfloat16 [16, 512, 2048], P('ep', 'edp'), may hold values from -0.59765625 to 0.59765625
Outputs:
- mixed: bfloat16 [4096, 2048], P(('edp', 'ep'))
- grad_gate: float32 [16, 2048, 768], P('ep', 'edp')
- grad_up: float32 [16, 2048, 768], P('ep', 'edp')
- grad_down: float32 [16, 768, 2048], P('ep', 'edp')
Inputs may be any that keep to these rules, and one draw needn't show every extreme that they name: `routes`: each token names 8 different experts. In each aligned block of 128 tokens (the tokens of one device) no expert is named more than 96 times, a bound that some block reaches in every draw.
All inputs are finite; a program needn't handle non-finite values.
Results may differ from a plain program's by a relative error of at most 0.006.
Values may be sent and summed in bfloat16 or wider, within the bound.
A program may use at most 128 MiB of HBM per device.

v0:
```python
import jax
import jax.numpy as jnp
from jax import lax
from jax.sharding import PartitionSpec as P


def expert_mlp(row_data, w_gate, w_up, w_down):
    gate_pre = jnp.dot(row_data, w_gate, preferred_element_type=jnp.float32)
    up_pre = jnp.dot(row_data, w_up, preferred_element_type=jnp.float32)
    hidden = (jax.nn.silu(gate_pre) * up_pre).astype(jnp.bfloat16)
    return jnp.dot(hidden, w_down, preferred_element_type=jnp.float32).astype(jnp.bfloat16)


def expert_grads(inputs, cotangent, w_gate, w_up, w_down):
    gate_pre = jnp.dot(inputs, w_gate, preferred_element_type=jnp.float32)
    up_pre = jnp.dot(inputs, w_up, preferred_element_type=jnp.float32)
    activated = jax.nn.silu(gate_pre)
    hidden = (activated * up_pre).astype(jnp.bfloat16)
    d_hidden = jnp.einsum("rd,fd->rf", cotangent, w_down, preferred_element_type=jnp.float32)
    sigmoid_gate = jax.nn.sigmoid(gate_pre)
    d_gate = (d_hidden * up_pre * sigmoid_gate * (1.0 + gate_pre * (1.0 - sigmoid_gate))).astype(
        jnp.bfloat16
    )
    d_up = (d_hidden * activated).astype(jnp.bfloat16)
    return (hidden, d_gate, d_up)


def rounded(value):
    return lax.optimization_barrier(value.astype(jnp.bfloat16)).astype(jnp.float32)


def dispatch_plan(routes, experts, capacity):
    route_flat = routes.reshape(-1)
    one_hot = (route_flat[:, None] == jnp.arange(experts, dtype=jnp.int32)[None, :]).astype(
        jnp.int32
    )
    running = jnp.cumsum(one_hot, axis=0) - 1
    slot_index = jnp.sum(running * one_hot, axis=1)
    return route_flat * capacity + slot_index


def shards(tokens, routes, gate_weights, w_gate, w_up, w_down, saved_inputs, saved_cotangent):
    experts = lax.axis_size("ep")
    tok_rows, width = tokens.shape
    top_count = routes.shape[1]
    capacity = 3 * tok_rows * top_count // (2 * experts)
    position = dispatch_plan(routes, experts, capacity)
    send_buffer = jnp.zeros((experts * capacity, width), jnp.bfloat16)
    send_buffer = send_buffer.at[position].set(jnp.repeat(tokens, top_count, axis=0))
    send_buffer = send_buffer.reshape(experts, capacity, width)
    gate_mat, up_mat, down_mat = (w_gate[0], w_up[0], w_down[0])
    received = lax.all_to_all(send_buffer, "ep", split_axis=0, concat_axis=0, tiled=True)
    output = expert_mlp(received.reshape(-1, width), gate_mat, up_mat, down_mat)
    returned = lax.all_to_all(
        output.reshape(received.shape), "ep", split_axis=0, concat_axis=0, tiled=True
    )
    picked = returned.reshape(experts * capacity, width)[position]
    weighted = (
        picked.astype(jnp.float32).reshape(tok_rows, top_count, width) * gate_weights[:, :, None]
    )
    combined = jnp.sum(weighted, axis=1).astype(jnp.bfloat16)
    all_inputs, all_cotangent = (
        lax.all_gather(saved_inputs, "edp", axis=1, tiled=True),
        lax.all_gather(saved_cotangent, "edp", axis=1, tiled=True),
    )
    replicas = lax.axis_size("edp")
    own_index = lax.axis_index("edp")
    row_block = saved_inputs.shape[1]
    half_width = width // replicas
    half_hidden = gate_mat.shape[1] // replicas
    grad_g = jnp.zeros((half_width, gate_mat.shape[1]), jnp.float32)
    grad_u = jnp.zeros((half_width, gate_mat.shape[1]), jnp.float32)
    grad_d = jnp.zeros((half_hidden, width), jnp.float32)
    for replica in range(replicas):
        inputs = all_inputs[0, replica * row_block : (replica + 1) * row_block]
        cotangent = all_cotangent[0, replica * row_block : (replica + 1) * row_block]
        hidden, d_gate, d_up = expert_grads(inputs, cotangent, gate_mat, up_mat, down_mat)
        in_cols = lax.dynamic_slice_in_dim(inputs, own_index * half_width, half_width, 1)
        hidden_cols = lax.dynamic_slice_in_dim(hidden, own_index * half_hidden, half_hidden, 1)
        grad_g = grad_g + rounded(
            jnp.einsum("rd,rf->df", in_cols, d_gate, preferred_element_type=jnp.float32)
        )
        grad_u = grad_u + rounded(
            jnp.einsum("rd,rf->df", in_cols, d_up, preferred_element_type=jnp.float32)
        )
        grad_d = grad_d + rounded(
            jnp.einsum("rf,rd->fd", hidden_cols, cotangent, preferred_element_type=jnp.float32)
        )
    grad_gate, grad_up, grad_down = (grad_g[None], grad_u[None], grad_d[None])
    return (combined, grad_gate, grad_up, grad_down)


def solution(mesh):
    return jax.shard_map(
        shards,
        mesh=mesh,
        in_specs=(
            P(("edp", "ep"), None),
            P(("edp", "ep"), None),
            P(("edp", "ep"), None),
            P("ep", None, None),
            P("ep", None, None),
            P("ep", None, None),
            P("ep", "edp", None),
            P("ep", "edp", None),
        ),
        out_specs=(
            P(("edp", "ep"), None),
            P("ep", "edp", None),
            P("ep", "edp", None),
            P("ep", "edp", None),
        ),
        check_vma=False,
    )
```

profile of v0, /device:TPU:11, one launch (start us, length us, event | category | flops | bytes accessed | tf_op | source)
XLA Modules:
  0.0 356.6 jit_solution(1685601165405335375)
XLA Ops:
  7.2 0.0 copy-start
  7.2 0.8 broadcast_multiply_fusion
  8.0 0.9 copy.16
  8.9 0.1 eq.29
  9.0 0.1 eq.25
  9.1 0.1 copy.15
  9.2 0.1 mul.87
  9.3 4.5 %reduce-window.6 = s32[16,8,128]{2,1,0:T(8,128)S(1)} reduce-window(s32[16,8,128]{2,1,0:T(8,128)S(1)} %fusion.43, s32[]{:T(128)} %constant.11.clone.1), window={size=1x1x128 pad=0_0x0_0x127_0}, to_apply=%region_0.0 | reduce-window | flops 2080768 | bytes 131076 | tf_op jit(solution)/shard_map/reduce-window
  13.8 0.1 slice.26
  13.9 0.1 copy.18
  14.1 0.1 copy.19
  14.2 0.1 add_add_fusion
  14.3 10.7 %scatter_custom_fusion = bf16[1536,2048]{1,0:T(8,128)(2,1)} fusion(s32[1024]{0:T(1024)S(1)} %bitcast.99, bf16[]{:T(256)} %constant.13.clone.1, bf16[128,2048]{1,0:T(8,128)(2,1)} %param.8), kind=kCustom, calls=%fused_computation.6 | custom fusion | bytes 6815746 | tf_op jit(solution)/shard_map/scatter | solution.py:49
  25.0 143.9 %all_to_all.10 = bf16[16,96,2048]{2,1,0:T(8,128)(2,1)S(1)} all-to-all(bf16[16,96,2048]{2,1,0:T(8,128)(2,1)} %bitcast.92), channel_id=1, replica_groups=mesh['edp'=2,'ep'=16] {'ep'}, dimensions={0} | all-to-all | bytes 12582912 | tf_op jit(solution)/shard_map/all_to_all | solution.py:52
  168.9 5.2 %fusion.17 = f32[1536,768]{1,0:T(8,128)S(1)} fusion(bf16[1536,2048]{1,0:T(8,128)(2,1)S(1)} %bitcast.94, bf16[1,2048,768]{2,1,0:T(8,128)(2,1)S(1)} %copy-done.4), kind=kOutput, calls=%fused_computation.22 | convolution fusion | flops 4831838208 | bytes 14155776 | tf_op jit(solution)/shard_map/dot_general | solution.py:8
  174.1 5.6 %multiply_convert_fusion = bf16[1536,768]{1,0:T(8,128)(2,1)S(1)} fusion(f32[1536,768]{1,0:T(8,128)S(1)} %fusion.17, bf16[1536,2048]{1,0:T(8,128)(2,1)S(1)} %bitcast.95, bf16[1,2048,768]{2,1,0:T(8,128)(2,1)S(1)} %copy-done.6), kind=kOutput, calls=%fused_computation.5 | convolution fusion | flops 4838916096 | bytes 16515072 | tf_op jit(solution)/shard_map/dot_general | solution.py:9
  179.7 7.0 %convolution_convert_fusion = bf16[1536,2048]{1,0:T(8,128)(2,1)} fusion(bf16[1536,768]{1,0:T(8,128)(2,1)S(1)} %multiply_convert_fusion, bf16[1,768,2048]{2,1,0:T(8,128)(2,1)S(1)} %copy-done), kind=kOutput, calls=%fused_computation.4 | convolution fusion | flops 4834983936 | bytes 11796480 | tf_op jit(solution)/shard_map/dot_general | solution.py:11
  186.8 5.5 %all-to-all-start.1 = ((bf16[16,96,2048]{2,1,0:T(8,128)(2,1)}), bf16[16,96,2048]{2,1,0:T(8,128)(2,1)}, u32[]{:S(2)}, u32[]{:S(2)}) async-start(bf16[16,96,2048]{2,1,0:T(8,128)(2,1)} %bitcast.93), calls=%async_computation.1 | async-start | bytes 12582912 | tf_op jit(solution)/shard_map/all_to_all | solution.py:54
  192.3 0.0 all-gather.5.cloned.1.call-start
  192.4 0.7 all-gather.5.cloned.1.call-update
  193.1 0.3 all-gather.3.cloned.1.call-start
  193.3 0.5 all-gather.3.cloned.1.call-update
  193.8 0.1 copy.20
  193.9 34.3 %all-gather.5.cloned.1.call-done = bf16[1,512,2048]{2,1,0:T(8,128)(2,1)} async-done(((bf16[1,256,2048]{2,1,0:T(8,128)(2,1)}), bf16[1,512,2048]{2,1,0:T(8,128)(2,1)}) %all-gather.5.cloned.1.call-update) | async-done | bytes 2097168 | tf_op jit(solution)/shard_map/all_gather | solution.py:64
  228.3 3.1 fusion.3
  231.4 31.5 %all-gather.3.cloned.1.call-done = bf16[1,512,2048]{2,1,0:T(8,128)(2,1)} async-done(((bf16[1,256,2048]{2,1,0:T(8,128)(2,1)}), bf16[1,512,2048]{2,1,0:T(8,128)(2,1)}) %all-gather.3.cloned.1.call-update) | async-done | bytes 2097168 | tf_op jit(solution)/shard_map/all_gather | solution.py:63
  262.9 3.4 fusion.25
  266.4 0.0 copy-start.8
  266.4 0.2 fusion.58
  266.6 0.9 copy-done.8
  267.5 0.7 convolution_convert_fusion.3
  268.2 0.1 copy-done.1
  268.3 1.0 fusion.5
  269.3 0.9 copy-done.5
  270.2 1.1 fusion.26
  271.3 0.7 convolution_convert_fusion.4
  271.9 1.2 copy-done.7
  273.1 1.0 fusion.8
  274.1 0.8 convolution_convert_fusion.5
  274.9 1.0 fusion.10
  275.9 0.8 convolution_convert_fusion.6
  276.7 0.6 convolution_convert_fusion.1
  277.3 0.6 convolution_convert_fusion.2
  278.0 3.4 add_bitcast_fusion.1
  281.4 2.3 add_bitcast_fusion
  283.6 46.1 %all-to-all-done.1 = bf16[16,96,2048]{2,1,0:T(8,128)(2,1)} async-done(((bf16[16,96,2048]{2,1,0:T(8,128)(2,1)}), bf16[16,96,2048]{2,1,0:T(8,128)(2,1)}, u32[]{:S(2)}, u32[]{:S(2)}) %all-to-all-start.1) | async-done | bytes 6291488 | tf_op jit(solution)/shard_map/all_to_all | solution.py:54
  329.7 12.7 %gather_fusion = bf16[1024,2048]{1,0:T(8,128)(2,1)} fusion(bf16[1536,2048]{1,0:T(8,128)(2,1)} %bitcast.11, s32[1024]{0:T(1024)S(1)} %broadcast_clamp_fusion), kind=kCustom, calls=%fused_computation | custom fusion | bytes 8392704 | tf_op jit(solution)/shard_map/gather | solution.py:57
  342.4 7.3 %fusion = bf16[128,2048]{1,0:T(8,128)(2,1)} fusion(bf16[1024,2048]{1,0:T(8,128)(2,1)} %gather_fusion, f32[128,8]{1,0:T(8,128)S(1)} %copy.20), kind=kLoop, calls=%fused_computation.3 | loop fusion | flops 6029312 | bytes 4722688 | tf_op jit(solution)/shard_map/reduce_sum | solution.py:61
  (18 shorter events, 0.1 us)
Async XLA Ops:
  7.2 172.6 %copy-start = (bf16[1,768,2048]{2,1,0:T(8,128)(2,1)S(1)}, bf16[1,768,2048]{2,1,0:T(8,128)(2,1)}, u32[]{:S(2)}) copy-start(bf16[1,768,2048]{2,1,0:T(8,128)(2,1)} %param.13) | copy-start | bytes 9437188
  25.0 143.9 %copy-start.4 = (bf16[1,2048,768]{2,1,0:T(8,128)(2,1)S(1)}, bf16[1,2048,768]{2,1,0:T(8,128)(2,1)}, u32[]{:S(2)}) copy-start(bf16[1,2048,768]{2,1,0:T(8,128)(2,1)} %param.11) | copy-start | bytes 9437188
  168.9 5.2 %copy-start.6 = (bf16[1,2048,768]{2,1,0:T(8,128)(2,1)S(1)}, bf16[1,2048,768]{2,1,0:T(8,128)(2,1)}, u32[]{:S(2)}) copy-start(bf16[1,2048,768]{2,1,0:T(8,128)(2,1)} %param.12) | copy-start | bytes 9437188
  186.8 7.0 %copy-start.3 = (f32[128,8]{0,1:T(8,128)S(1)}, f32[128,8]{0,1:T(8,128)}, u32[]{:S(2)}) copy-start(f32[128,8]{0,1:T(8,128)} %param.10) | copy-start | bytes 12292
  186.8 143.0 %all-to-all-start.1 = ((bf16[16,96,2048]{2,1,0:T(8,128)(2,1)}), bf16[16,96,2048]{2,1,0:T(8,128)(2,1)}, u32[]{:S(2)}, u32[]{:S(2)}) async-start(bf16[16,96,2048]{2,1,0:T(8,128)(2,1)} %bitcast.93), calls=%async_computation.1 | async-start | bytes 12582912 | tf_op jit(solution)/shard_map/all_to_all | solution.py:54
  192.3 35.9 %all-gather.5.cloned.1.call-start = ((), (), s32[]{:S(2)}) async-start(), calls=%async_computation.3 | async-start | bytes 3145728 | tf_op jit(solution)/shard_map/all_gather | solution.py:64
  193.1 69.9 %all-gather.3.cloned.1.call-start = ((), (), s32[]{:S(2)}) async-start(), calls=%async_computation.2 | async-start | bytes 3145728 | tf_op jit(solution)/shard_map/all_gather | solution.py:63
  262.9 3.4 copy-start.2
  266.4 1.1 copy-start.8
  266.6 1.7 copy-start.1
  268.3 1.9 copy-start.5
  271.2 1.9 copy-start.7
Sparse Core Ops, SparseCore 0:
  194.7 33.5 all-gather.4
  229.8 33.0 all-gather.2
where the time goes:
time: 357 us
  blocking collectives  144 us (40%)
  waiting for transfers between devices  113 us (32%)
  matrix products  32.6 us (9%)
  local copies, waits for them, and re-layouts  28.3 us (8%)
  other arithmetic  18.5 us (5%)
  between operations  14.3 us (4%)
  starting transfers between devices  5.84 us (2%)
    all_to_all x1, blocking collectives, shards(): lax.all_to_all(send_buffer, 'ep', split_axis=0, concat_axis=0, tiled=True)  144 us
    all_to_all x1, waiting for transfers between devices, shards(): lax.all_to_all(output.reshape(received.shape), 'ep', split_axis=0, concat...  46.1 us
    all_gather x1, waiting for transfers between devices, shards(): lax.all_gather(saved_cotangent, 'edp', axis=1, tiled=True)  34.3 us
    all_gather x1, waiting for transfers between devices, shards(): lax.all_gather(saved_inputs, 'edp', axis=1, tiled=True)  31.5 us
    gather x1, local copies, waits for them, and re-layouts, shards(): picked = returned.reshape(experts * capacity, width)[position]  12.7 us
    scatter x1, local copies, waits for them, and re-layouts, shards(): send_buffer.at[position].set(jnp.repeat(tokens, top_count, axis=0))  10.7 us
    reduce_sum x1, other arithmetic, shards(): combined = jnp.sum(weighted, axis=1).astype(jnp.bfloat16)  7.32 us
  transfers between devices with their start and end apart: 3, of which 3 were waited for; matrix products, arithmetic and copies ran while one was open for 6% of the time, Pallas kernels for 0%

commit v1 on v0

v1 whole, which is shorter than its diff:
```python
import functools

import jax
import jax.numpy as jnp
from jax import lax
from jax.experimental import pallas as pl
from jax.experimental.pallas import tpu as pltpu
from jax.sharding import PartitionSpec as P

MESH = pl.DeviceIdType.MESH


def place():
    index = lax.axis_index("ep")
    return index, index // 4, (index // 2) % 2, index % 2


def gather_kernel(
    line, tok, tab, inp, cot, tok_o, tab_o, inp_o, cot_o,
    local, up_s, down_s, line_r, pair_s, pair_r, core_s, core_r, rep_s, rep_r,
):
    index, z, x, c = place()
    rep = lax.axis_index("edp")
    pair_dev = index + 2 - 4 * x
    core_dev = index + 1 - 2 * c

    def block(zz, xx, cc):
        return (zz * 2 + xx) * 2 + cc

    def copies(blk, own, target, send, recv, slot):
        out = []
        for k, (first, array) in enumerate(((tok, tok_o), (tab, tab_o))):
            out.append(
                pltpu.make_async_remote_copy(
                    src_ref=first if own else array.at[blk],
                    dst_ref=array.at[blk],
                    send_sem=send.at[slot, k],
                    recv_sem=recv.at[slot, k],
                    device_id={"ep": target},
                    device_id_type=MESH,
                )
            )
        return out

    def up(zz, own):
        return copies(block(zz, x, c), own, index + 4, up_s, line_r, zz)

    def down(zz, own):
        return copies(block(zz, x, c), own, index - 4, down_s, line_r, zz)

    def pair(zz, own, xx):
        return copies(block(zz, xx, c), own, pair_dev, pair_s, pair_r, zz)

    def core(zz, xx, own, cc):
        return copies(block(zz, xx, cc), own, core_dev, core_s, core_r, zz * 2 + xx)

    def start(items):
        for item in items:
            item.start()

    def landed(items):
        for item in items:
            item.wait_recv()

    def sent(items):
        for item in items:
            item.wait_send()

    def replica(k):
        other = 1 - rep
        source, target = ((inp, inp_o), (cot, cot_o))[k]
        return pltpu.make_async_remote_copy(
            src_ref=source,
            dst_ref=target.at[rep],
            send_sem=rep_s.at[k],
            recv_sem=rep_r.at[k],
            device_id={"edp": other},
            device_id_type=MESH,
        )

    keep = [
        pltpu.make_async_copy(tok, tok_o.at[index], local.at[0]),
        pltpu.make_async_copy(tab, tab_o.at[index], local.at[1]),
        pltpu.make_async_copy(inp, inp_o.at[rep], local.at[2]),
        pltpu.make_async_copy(cot, cot_o.at[rep], local.at[3]),
    ]

    @pl.when(z < line - 1)
    def _():
        start(up(z, True))

    @pl.when(z > 0)
    def _():
        start(down(z, True))

    start(pair(z, True, x))
    replica(0).start()
    replica(1).start()
    start(core(z, x, True, c))
    start(keep)

    def from_pair(zz):
        landed(pair(zz, False, 1 - x))
        start(core(zz, 1 - x, False, c))

    for d in range(1, line + 1):
        if d < line:

            @pl.when(z >= d)
            def _(d=d):
                landed(up(z - d, False))

                @pl.when(z < line - 1)
                def _():
                    start(up(z - d, False))

                start(pair(z - d, False, x))
                start(core(z - d, x, False, c))

            @pl.when(z + d < line)
            def _(d=d):
                landed(down(z + d, False))

                @pl.when(z > 0)
                def _():
                    start(down(z + d, False))

                start(pair(z + d, False, x))
                start(core(z + d, x, False, c))

        e = d - 1
        if e == 0:
            from_pair(z)
        else:

            @pl.when(z >= e)
            def _(e=e):
                from_pair(z - e)

            @pl.when(z + e < line)
            def _(e=e):
                from_pair(z + e)

    for zz in range(line):
        for xx in range(2):
            landed(core(zz, xx, False, 1 - c))
            sent(core(zz, xx, False, c))
        sent(pair(zz, False, x))

        @pl.when((z >= zz) & (z < line - 1))
        def _(zz=zz):
            sent(up(zz, False))

        @pl.when((z <= zz) & (z > 0))
        def _(zz=zz):
            sent(down(zz, False))

    for k in range(2):
        replica(k).wait()
    for item in keep:
        item.wait()


def gather(tokens, table, inputs, cotangent):
    size = lax.axis_size("ep")
    replicas = lax.axis_size("edp")
    line = size // 4
    dma = pltpu.SemaphoreType.DMA
    return pl.pallas_call(
        functools.partial(gather_kernel, line),
        out_shape=(
            jax.ShapeDtypeStruct((size,) + tokens.shape, tokens.dtype),
            jax.ShapeDtypeStruct((size,) + table.shape, table.dtype),
            jax.ShapeDtypeStruct((replicas,) + inputs.shape, inputs.dtype),
            jax.ShapeDtypeStruct((replicas,) + cotangent.shape, cotangent.dtype),
        ),
        in_specs=[pl.BlockSpec(memory_space=pltpu.VMEM)] * 4,
        out_specs=(pl.BlockSpec(memory_space=pl.ANY),) * 4,
        scratch_shapes=[
            dma((4,)),
            dma((line, 2)),
            dma((line, 2)),
            dma((line, 2)),
            dma((line, 2)),
            dma((line, 2)),
            dma((line * 2, 2)),
            dma((line * 2, 2)),
            dma((2,)),
            dma((2,)),
        ],
        compiler_params=pltpu.CompilerParams(has_side_effects=True),
        name="gather",
    )(tokens, table, inputs, cotangent)


def reduce_kernel(
    line, part, out, own, rc, sx, rx, ru, rd, su, sd, acc,
    local, core_s, core_r, pair_s, pair_r, up_s, up_r, down_s, down_r,
):
    index, z, x, c = place()
    pair_dev = index + 2 - 4 * x
    core_dev = index + 1 - 2 * c
    rows = out.shape[0]

    def remote(src, dst, send, recv, target, slot):
        return pltpu.make_async_remote_copy(
            src_ref=src, dst_ref=dst, send_sem=send.at[slot], recv_sem=recv.at[slot],
            device_id={"ep": target}, device_id_type=MESH,
        )

    def core(t, xx):
        slot = t * 2 + xx
        return remote(part.at[slot * 2 + 1 - c], rc.at[slot], core_s, core_r, core_dev, slot)

    def load(t, xx):
        slot = t * 2 + xx
        return pltpu.make_async_copy(part.at[slot * 2 + c], own.at[slot], local.at[slot])

    def pair(t):
        return remote(sx.at[t], rx.at[t], pair_s, pair_r, pair_dev, t)

    def up(t):
        return remote(su.at[t], ru.at[t], up_s, up_r, index + 4, t)

    def down(t):
        return remote(sd.at[t], rd.at[t], down_s, down_r, index - 4, t)

    def each_target(body):
        for d in range(line - 1, 0, -1):

            @pl.when(z + d < line)
            def _(d=d):
                body(z + d, 1)

            @pl.when(z >= d)
            def _(d=d):
                body(z - d, -1)

        body(z, 0)

    def slabs(step):
        def one(i, carry):
            step(pl.ds(pl.multiple_of(i * 16, 16), 16))
            return carry

        lax.fori_loop(0, rows // 16, one, 0)

    def base(t, xx):
        slot = t * 2 + xx
        load(t, xx).wait()
        core(t, xx).wait_recv()
        return slot

    def begin(xx):
        def body(t, side):
            core(t, xx).start()
            load(t, xx).start()

        return body

    each_target(begin(1 - x))
    each_target(begin(x))

    def cross(t, side):
        slot = base(t, 1 - x)

        def step(r):
            total = own[slot, r, :].astype(jnp.float32) + rc[slot, r, :].astype(jnp.float32)
            sx[t, r, :] = total.astype(jnp.bfloat16)

        slabs(step)
        pair(t).start()

    each_target(cross)

    def join(source, t):
        def step(r):
            acc[r, :] += source[t, r, :].astype(jnp.float32)

        slabs(step)

    def along(t, side):
        slot = base(t, x)
        pair(t).wait_recv()

        def step(r):
            total = own[slot, r, :].astype(jnp.float32) + rc[slot, r, :].astype(jnp.float32)
            acc[r, :] = total + rx[t, r, :].astype(jnp.float32)

        slabs(step)
        if side >= 0:

            @pl.when(z > 0)
            def _():
                up(t).wait_recv()
                join(ru, t)

        if side <= 0:

            @pl.when(z < line - 1)
            def _():
                down(t).wait_recv()
                join(rd, t)

        def finish(r):
            value = acc[r, :].astype(jnp.bfloat16)
            if side > 0:
                su[t, r, :] = value
            elif side < 0:
                sd[t, r, :] = value
            else:
                out[r, :] = value

        slabs(finish)
        if side > 0:
            up(t).start()
        elif side < 0:
            down(t).start()

    each_target(along)

    def drain(t, side):
        core(t, 0).wait_send()
        core(t, 1).wait_send()
        pair(t).wait_send()
        if side > 0:
            up(t).wait_send()
        elif side < 0:
            down(t).wait_send()

    each_target(drain)


def reduce(partial):
    size, rows, width = partial.shape
    line = size // 4
    dma = pltpu.SemaphoreType.DMA

    def slots(count):
        return pltpu.VMEM((count, rows, width), partial.dtype)

    return pl.pallas_call(
        functools.partial(reduce_kernel, line),
        out_shape=jax.ShapeDtypeStruct((rows, width), partial.dtype),
        in_specs=[pl.BlockSpec(memory_space=pl.ANY)],
        out_specs=pl.BlockSpec(memory_space=pltpu.VMEM),
        scratch_shapes=[slots(line * 2), slots(line * 2)]
        + [slots(line) for _ in range(6)]
        + [pltpu.VMEM((rows, width), jnp.float32)]
        + [dma((line * 2,))] * 3
        + [dma((line,))] * 6,
        compiler_params=pltpu.CompilerParams(has_side_effects=True, vmem_limit_bytes=40 << 20),
        name="reduce",
    )(partial)


def expert_mlp(row_data, w_gate, w_up, w_down):
    gate_pre = jnp.dot(row_data, w_gate, preferred_element_type=jnp.float32)
    up_pre = jnp.dot(row_data, w_up, preferred_element_type=jnp.float32)
    hidden = (jax.nn.silu(gate_pre) * up_pre).astype(jnp.bfloat16)
    return jnp.dot(hidden, w_down, preferred_element_type=jnp.float32)


def expert_grads(inputs, cotangent, w_gate, w_up, w_down):
    gate_pre = jnp.dot(inputs, w_gate, preferred_element_type=jnp.float32)
    up_pre = jnp.dot(inputs, w_up, preferred_element_type=jnp.float32)
    activated = jax.nn.silu(gate_pre)
    hidden = (activated * up_pre).astype(jnp.bfloat16)
    d_hidden = jnp.einsum("rd,fd->rf", cotangent, w_down, preferred_element_type=jnp.float32)
    sigmoid_gate = jax.nn.sigmoid(gate_pre)
    d_gate = (d_hidden * up_pre * sigmoid_gate * (1.0 + gate_pre * (1.0 - sigmoid_gate))).astype(
        jnp.bfloat16
    )
    d_up = (d_hidden * activated).astype(jnp.bfloat16)
    return (hidden, d_gate, d_up)


def shards(tokens, routes, gate_weights, w_gate, w_up, w_down, saved_inputs, saved_cotangent):
    experts = lax.axis_size("ep")
    tok_rows, width = tokens.shape
    gate_mat, up_mat, down_mat = (w_gate[0], w_up[0], w_down[0])
    hit = routes[None, :, :] == jnp.arange(experts, dtype=jnp.int32)[:, None, None]
    table = jnp.sum(jnp.where(hit, gate_weights[None], 0.0), axis=2)
    kernels = experts % 4 == 0 and experts <= 16 and lax.axis_size("edp") == 2
    if kernels:
        all_tokens, all_table, all_inputs, all_cotangent = gather(
            tokens, table, saved_inputs[0], saved_cotangent[0]
        )
        all_inputs = all_inputs.reshape(-1, width)
        all_cotangent = all_cotangent.reshape(-1, width)
        mine = lax.dynamic_index_in_dim(all_table, lax.axis_index("ep"), 1, keepdims=False)
    else:
        all_tokens = lax.all_gather(tokens, "ep", axis=0)
        mine = lax.all_to_all(table, "ep", split_axis=0, concat_axis=0, tiled=True)
        all_inputs = lax.all_gather(saved_inputs[0], "edp", axis=0, tiled=True)
        all_cotangent = lax.all_gather(saved_cotangent[0], "edp", axis=0, tiled=True)
    output = expert_mlp(all_tokens.reshape(-1, width), gate_mat, up_mat, down_mat)
    partial = (output * mine.reshape(-1, 1)).astype(jnp.bfloat16)
    if kernels:
        combined = reduce(partial.reshape(experts, tok_rows, width))
    else:
        combined = lax.psum_scatter(partial, "ep", scatter_dimension=0, tiled=True)

    replicas = lax.axis_size("edp")
    own_index = lax.axis_index("edp")
    half_width = width // replicas
    half_hidden = gate_mat.shape[1] // replicas
    hidden, d_gate, d_up = expert_grads(all_inputs, all_cotangent, gate_mat, up_mat, down_mat)
    in_cols = lax.dynamic_slice_in_dim(all_inputs, own_index * half_width, half_width, 1)
    hidden_cols = lax.dynamic_slice_in_dim(hidden, own_index * half_hidden, half_hidden, 1)
    grad_g = jnp.einsum("rd,rf->df", in_cols, d_gate, preferred_element_type=jnp.float32)
    grad_u = jnp.einsum("rd,rf->df", in_cols, d_up, preferred_element_type=jnp.float32)
    grad_d = jnp.einsum("rf,rd->fd", hidden_cols, all_cotangent, preferred_element_type=jnp.float32)
    return (combined, grad_g[None], grad_u[None], grad_d[None])


def solution(mesh):
    return jax.shard_map(
        shards,
        mesh=mesh,
        in_specs=(
            P(("edp", "ep"), None),
            P(("edp", "ep"), None),
            P(("edp", "ep"), None),
            P("ep", None, None),
            P("ep", None, None),
            P("ep", None, None),
            P("ep", "edp", None),
            P("ep", "edp", None),
        ),
        out_specs=(
            P(("edp", "ep"), None),
            P("ep", "edp", None),
            P("ep", "edp", None),
            P("ep", "edp", None),
        ),
        check_vma=False,
    )
```

time: 357 us -> 183 us (0.51)
  the two profiles are of different devices: /device:TPU:11 before, /device:TPU:0 now
where the time goes in v1:
time: 183 us
  Pallas kernels  122 us (67%)
  matrix products  52.2 us (29%)
  local copies, waits for them, and re-layouts  6.46 us (4%)
    pallas_call x1, Pallas kernels, gather(): pl.pallas_call(functools.partial(gather_kernel, line), out_shape=(jax.Sha...  64.9 us
    pallas_call x1, Pallas kernels, reduce(): pl.pallas_call(functools.partial(reduce_kernel, line), out_shape=jax.Shap...  57 us
    dot_general x1, matrix products, expert_mlp(): return jnp.dot(hidden, w_down, preferred_element_type=jnp.float32)  20.6 us
    dot_general x1, matrix products, expert_mlp(): gate_pre = jnp.dot(row_data, w_gate, preferred_element_type=jnp.float32)  11.7 us
    dot_general x1, matrix products, expert_grads(): gate_pre = jnp.dot(inputs, w_gate, preferred_element_type=jnp.float32)  5.75 us
    unnamed x17, local copies, waits for them, and re-layouts  5.61 us
    dot_general x1, matrix products, shards(): jnp.einsum('rf,rd->fd', hidden_cols, all_cotangent, preferred_element_typ...  4.8 us

profile of v1, /device:TPU:0, one launch (start us, length us, event | category | flops | bytes accessed | tf_op | source)
XLA Modules:
  0.0 182.8 jit_solution(13772626798829517272)
XLA Ops:
  0.6 0.0 copy-start
  0.6 1.5 select_reduce_fusion.tab
  2.1 64.9 %gather.1 = (bf16[16,128,2048]{2,1,0:T(8,128)(2,1)}, f32[16,16,128]{2,1,0:T(8,128)}, bf16[2,256,2048]{2,1,0:T(8,128)(2,1)}, bf16[2,256,2048]{2,1,0:T(8,128)(2,1)}) custom-call(bf16[128,2048]{1,0:T(8,128)(2,1)} %tok.1, f32[16,128]{1,0:T(8,128)} %select_reduce_fusion.tab, bf16[256,2048]{1,0:T(8,128)(2,1)} %bitcast.40, bf16[256,2048]{1,0:T(8,128)(2,1)} %bitcast.41), custom_call_target="tpu_custom_call" | custom-call | tf_op jit(solution)/shard_map/gather/pallas_call | solution.py:169
  67.0 0.9 constant_dynamic-slice_fusion
  67.9 11.7 %fusion.9 = f32[2048,768]{1,0:T(8,128)} fusion(bf16[2048,2048]{1,0:T(8,128)(2,1)} %bitcast.43, bf16[1,2048,768]{2,1,0:T(8,128)(2,1)} %param.11), kind=kOutput, calls=%fused_computation.10 | convolution fusion | flops 6442450944 | bytes 17825792 | tf_op jit(solution)/shard_map/dot_general | solution.py:358
  79.6 0.0 copy-done
  79.6 20.6 %multiply_convert_fusion = bf16[2048,2048]{1,0:T(8,128)(2,1)} fusion(f32[2048]{0:T(1024)S(1)} %bitcast.42, f32[2048,768]{1,0:T(8,128)} %fusion.9, bf16[2048,2048]{1,0:T(8,128)(2,1)} %bitcast.44, bf16[1,768,2048]{2,1,0:T(8,128)(2,1)S(1)} %copy-done, bf16[1,2048,768]{2,1,0:T(8,128)(2,1)} %param.12), kind=kOutput, calls=%fused_computation | convolution fusion | flops 12902727680 | bytes 29368320 | tf_op jit(solution)/shard_map/dot_general | solution.py:361
  100.2 0.0 copy-start.1
  100.2 3.4 %copy-done.1 = bf16[2048,2048]{1,0:T(8,128)(2,1)S(1)} copy-done((bf16[2048,2048]{1,0:T(8,128)(2,1)S(1)}, bf16[2048,2048]{1,0:T(8,128)(2,1)}, u32[]{:S(2)}) %copy-start.1) | copy-done | bytes 8388632
  103.5 57.0 %reduce.1 = bf16[128,2048]{1,0:T(8,128)(2,1)S(1)} custom-call(bf16[16,128,2048]{2,1,0:T(8,128)(2,1)S(1)} %bitcast.37), custom_call_target="tpu_custom_call" | custom-call | tf_op jit(solution)/shard_map/reduce/pallas_call | solution.py:342
  160.6 0.0 copy-start.2
  160.6 0.8 copy-done.2
  161.4 0.0 copy-start.4
  161.4 5.7 %fusion.12 = (f32[512,768]{1,0:T(8,128)}, f32[512,768]{1,0:T(8,128)S(1)}) fusion(bf16[512,2048]{1,0:T(8,128)(2,1)} %bitcast.45, bf16[1,2048,768]{2,1,0:T(8,128)(2,1)} %param.11), kind=kOutput, calls=%fused_computation.19 | convolution fusion | flops 1612185600 | bytes 8388608 | tf_op jit(solution)/shard_map/dot_general | solution.py:365
  167.1 0.0 copy-done.4
  167.1 0.0 copy-start.6
  167.1 0.0 copy-start.7
  167.1 1.9 %fusion = f32[512,768]{1,0:T(8,128)S(1)} fusion(bf16[512,2048]{1,0:T(8,128)(2,1)S(1)} %bitcast.39, bf16[1,768,2048]{2,1,0:T(8,128)(2,1)S(1)} %copy-done), kind=kOutput, calls=%fused_computation.2 | convolution fusion | flops 1610612736 | bytes 6815744 | tf_op jit(solution)/shard_map/rd,fd->rf/dot_general | solution.py:369
  169.0 0.0 copy-done.6
  169.1 0.6 copy-done.7
  169.7 1.8 fusion.3
  171.5 0.0 copy-start.5
  171.5 2.9 %convolution_bitcast_fusion.2 = f32[1,1024,768]{2,1,0:T(8,128)} fusion(bf16[512,2048]{1,0:T(8,128)(2,1)S(1)} %bitcast.47, s32[]{:T(128)S(6)} %select_n.16, f32[512,768]{1,0:T(8,128)S(1)} %get-tuple-element.13, f32[512,768]{1,0:T(8,128)S(1)} %fusion, f32[512,768]{1,0:T(8,128)S(1)} %fusion.3), kind=kOutput, calls=%fused_computation.15 | convolution fusion | flops 809238528 | bytes 8912900 | tf_op jit(solution)/shard_map/rd,rf->df/dot_general | solution.py:411
  174.4 0.0 copy-done.5
  174.4 2.8 %convolution_bitcast_fusion.1 = f32[1,1024,768]{2,1,0:T(8,128)} fusion(bf16[512,2048]{1,0:T(8,128)(2,1)S(1)} %bitcast.48, s32[]{:T(128)S(6)} %select_n.16, f32[512,768]{1,0:T(8,128)S(1)} %fusion, f32[512,768]{1,0:T(8,128)S(1)} %get-tuple-element.13), kind=kOutput, calls=%fused_computation.14 | convolution fusion | flops 807665664 | bytes 7340036 | tf_op jit(solution)/shard_map/rd,rf->df/dot_general | solution.py:412
  177.2 0.0 copy-start.3
  177.2 4.8 %convolution_bitcast_fusion = f32[1,384,2048]{2,1,0:T(8,128)} fusion(bf16[512,2048]{1,0:T(8,128)(2,1)} %bitcast.38, f32[512,768]{1,0:T(8,128)} %copy-done.5, s32[]{:T(128)S(6)} %select_n.17, f32[512,768]{1,0:T(8,128)} %get-tuple-element.12), kind=kOutput, calls=%fused_computation.13 | convolution fusion | flops 805699584 | bytes 6815748 | tf_op jit(solution)/shard_map/rf,rd->fd/dot_general | solution.py:413
  182.0 0.0 copy-done.3
  182.0 0.8 copy.15
Async XLA Ops:
  0.6 78.9 %copy-start = (bf16[1,768,2048]{2,1,0:T(8,128)(2,1)S(1)}, bf16[1,768,2048]{2,1,0:T(8,128)(2,1)}, u32[]{:S(2)}) copy-start(bf16[1,768,2048]{2,1,0:T(8,128)(2,1)} %param.13) | copy-start | bytes 9437188
  100.2 3.4 %copy-start.1 = (bf16[2048,2048]{1,0:T(8,128)(2,1)S(1)}, bf16[2048,2048]{1,0:T(8,128)(2,1)}, u32[]{:S(2)}) copy-start(bf16[2048,2048]{1,0:T(8,128)(2,1)} %multiply_convert_fusion) | copy-start | bytes 25165828
  160.6 0.8 copy-start.2
  161.4 5.8 %copy-start.4 = (bf16[2,256,2048]{2,1,0:T(8,128)(2,1)S(1)}, bf16[2,256,2048]{2,1,0:T(8,128)(2,1)}, u32[]{:S(2)}) copy-start(bf16[2,256,2048]{2,1,0:T(8,128)(2,1)} %get-tuple-element.11) | copy-start | bytes 6291460
  167.1 1.9 %copy-start.6 = (bf16[1,2048,768]{2,1,0:T(8,128)(2,1)S(1)}, bf16[1,2048,768]{2,1,0:T(8,128)(2,1)}, u32[]{:S(2)}) copy-start(bf16[1,2048,768]{2,1,0:T(8,128)(2,1)} %param.12) | copy-start | bytes 9437188
  167.1 2.5 %copy-start.7 = (bf16[2,256,2048]{2,1,0:T(8,128)(2,1)S(1)}, bf16[2,256,2048]{2,1,0:T(8,128)(2,1)}, u32[]{:S(2)}) copy-start(bf16[2,256,2048]{2,1,0:T(8,128)(2,1)} %get-tuple-element.10) | copy-start | bytes 6291460
  171.5 2.9 %copy-start.5 = (f32[512,768]{1,0:T(8,128)}, f32[512,768]{1,0:T(8,128)S(1)}, u32[]{:S(2)}) copy-start(f32[512,768]{1,0:T(8,128)S(1)} %fusion.3) | copy-start | bytes 4718596
  177.2 4.8 %copy-start.3 = (bf16[128,2048]{1,0:T(8,128)(2,1)S(1)}, bf16[128,2048]{1,0:T(8,128)(2,1)}, u32[]{:S(2)}) copy-start(bf16[128,2048]{1,0:T(8,128)(2,1)} %copy-done.2) | copy-start | bytes 1572868
